TPU v7x, 32 devices: a whole 2x2x4 slice. The times are simulated.
32 devices in a mesh: ex: 4 (over y, x), ft: 8 (over z, core).
Axes of the slice: x: 2, y: 2, z: 4, core: 2. Of those that a mesh axis runs over, the one named last changes fastest.
Arguments:
- features: bfloat16 [512, 262144], P(('ex', 'ft')), may hold values from -0.0234375 to 0.0234375
- labels: int32 [512], P(('ex', 'ft')), may hold values 0 or 1
- start_weights: float32 [262144], P(('ex', 'ft')), may hold values from -6 to 6
- hist_s: float32 [20, 262144], P(None, ('ex', 'ft')), may hold values from -12 to 12
- hist_y: float32 [20, 262144], P(None, ('ex', 'ft')), may hold values from -30 to 30, as said below
Outputs:
- new_weights: float32 [262144], P(('ex', 'ft'))
- direction: float32 [262144], P(('ex', 'ft'))
Inputs may be any that keep to these rules, and one draw needn't show every extreme that they name: Entry by entry, hist_y times hist_s is nonnegative, and every pair has a positive inner product; every entry of hist_y is at most 1.2 times the matching entry of hist_s in magnitude.
All inputs are finite; a program needn't handle non-finite values. No bound on the sum of `labels` on one device may be relied on, other than what follows from the above.
Results may differ from a plain program's by a relative error of at most 0.0081.
Values may be sent and summed in bfloat16 or wider, within the bound.
A program may use at most 64 MiB of HBM per device.

v0:
```python
import jax
import jax.numpy as jnp
from jax import lax
from jax.sharding import PartitionSpec as P

ITERS = 2


def two_loop(gram):
    pairs = (gram.shape[0] - 1) // 2
    delta = jnp.zeros((gram.shape[0],), jnp.float32).at[2 * pairs].set(-1.0)
    alphas = [None] * pairs
    for index in reversed(range(pairs)):
        alpha = jnp.sum(delta * gram[:, index]) / gram[index, pairs + index]
        delta = delta.at[pairs + index].add(-alpha)
        alphas[index] = alpha
    delta = delta * (gram[pairs - 1, 2 * pairs - 1] / gram[2 * pairs - 1, 2 * pairs - 1])
    for index in range(pairs):
        beta = jnp.sum(delta * gram[pairs + index, :]) / gram[index, pairs + index]
        delta = delta.at[index].add(alphas[index] - beta)
    return delta


def local_gram(left, basis):
    return jnp.dot(
        left, basis.T, precision=lax.Precision.HIGHEST, preferred_element_type=jnp.float32
    )


def per_device(features, labels, start_weights, hist_s, hist_y):
    pairs = hist_s.shape[0]
    weights = start_weights
    stored_s, stored_y = (hist_s, hist_y)
    prev_weights = weights
    prev_grad = weights
    direction = weights
    gram = jnp.zeros((2 * pairs + 1, 2 * pairs + 1), jnp.float32)
    for step in range(ITERS):
        half_weights = weights.astype(jnp.bfloat16)
        margins_quarter = lax.all_gather(half_weights, "ft", axis=0, tiled=True)
        margin = jnp.dot(
            features,
            lax.all_gather(margins_quarter, "ex", axis=0, tiled=True),
            preferred_element_type=jnp.float32,
        )
        resid = (jax.nn.sigmoid(margin) - labels.astype(jnp.float32)).astype(jnp.bfloat16)
        quarter = lax.psum_scatter(
            jnp.dot(resid, features, preferred_element_type=jnp.float32),
            "ex",
            scatter_dimension=0,
            tiled=True,
        )
        summed = lax.psum_scatter(quarter, "ft", scatter_dimension=0, tiled=True)
        grad = summed + 0.1 * weights
        if step > 0:
            stored_s = jnp.concatenate([stored_s[1:], (weights - prev_weights)[None]], axis=0)
            stored_y = jnp.concatenate([stored_y[1:], (grad - prev_grad)[None]], axis=0)
        basis = jnp.concatenate([stored_s, stored_y, grad[None]], axis=0)
        gram = lax.psum(local_gram(basis, basis), ("ex", "ft"))
        delta = two_loop(gram)
        direction = jnp.dot(
            delta, basis, precision=lax.Precision.HIGHEST, preferred_element_type=jnp.float32
        )
        prev_weights, prev_grad = (weights, grad)
        weights = weights + direction
    return (weights, direction)


def solution(mesh):
    return jax.shard_map(
        per_device,
        mesh=mesh,
        in_specs=(
            P(("ex", "ft"), None),
            P(("ex", "ft")),
            P(("ex", "ft")),
            P(None, ("ex", "ft")),
            P(None, ("ex", "ft")),
        ),
        out_specs=(P(("ex", "ft")), P(("ex", "ft"))),
        check_vma=False,
    )
```

profile of v0, /device:TPU:0, one launch (start us, length us, event | category | flops | bytes accessed | tf_op | source)
XLA Modules:
  0.0 564.3 jit_solution(57838217140362388)
XLA Ops:
  7.2 0.8 convert_element_type.16
  8.0 15.7 %all_gather.12 = bf16[65536]{0:T(1024)(128)(2,1)S(1)} all-gather(bf16[8192]{0:T(1024)(128)(2,1)S(1)} %convert_element_type.16), channel_id=1, replica_groups=mesh['ex'=4,'ft'=8] {'ft'}, dimensions={0}, use_global_device_ids=true | all-gather | bytes 147456 | tf_op jit(solution)/shard_map/all_gather | solution.py:40
  23.7 10.3 %all_gather.13 = bf16[262144]{0:T(1024)(128)(2,1)S(1)} all-gather(bf16[65536]{0:T(1024)(128)(2,1)S(1)} %all_gather.12), channel_id=1, replica_groups=mesh['ex'=4,'ft'=8] {'ex'}, dimensions={0}, use_global_device_ids=true | all-gather | bytes 655360 | tf_op jit(solution)/shard_map/all_gather | solution.py:43
  34.6 6.9 %fusion.8 = bf16[16,1]{0,1:T(2,128)(2,1)S(1)} fusion(bf16[16,262144]{1,0:T(8,128)(2,1)} %param.169, bf16[262144,1]{0,1:T(2,128)(2,1)S(1)} %reshape.1755, s32[16]{0:T(128)S(1)} %copy-done.5), kind=kOutput, calls=%fused_computation.11 | convolution fusion | flops 8388704 | bytes 8912992 | tf_op jit(solution)/shard_map/dot_general | solution.py:41
  41.6 2.4 fusion.109
  45.4 51.3 %all-reduce.9.cloned.1.call-done = f32[262144]{0:T(1024)} async-done(((f32[262144]{0:T(1024)}), f32[262144]{0:T(1024)}) %all-reduce.9.cloned.1.call-update) | async-done | bytes 1048592
  96.7 1.7 dynamic-slice.490
  99.7 54.8 %all-reduce.11.cloned.1.call-done = f32[65536]{0:T(1024)} async-done(((f32[65536]{0:T(1024)}), f32[65536]{0:T(1024)}) %all-reduce.11.cloned.1.call-update) | async-done | bytes 262160
  154.5 0.8 dynamic-slice_add_fusion.1
  155.3 1.4 fusion.15
  156.7 39.5 %psum.14 = f32[41,41]{1,0:T(8,128)S(1)} all-reduce(f32[41,41]{1,0:T(8,128)S(1)} %fusion.15), channel_id=1, replica_groups=mesh['ex'=4,'ft'=8] {'ex','ft'}, use_global_device_ids=true, to_apply=%region_2.0 | all-reduce | flops 1681 | bytes 13448 | tf_op jit(solution)/shard_map/psum | solution.py:59
  196.2 0.7 fusion.108
  197.4 0.7 fusion.107
  198.1 0.7 fusion.17
  242.8 0.6 fusion.95
  244.9 0.6 fusion.93
  246.9 0.6 fusion.91
  251.0 0.6 fusion.87
  253.1 0.6 fusion.85
  255.1 0.6 fusion.83
  257.3 0.6 fusion.81
  259.3 0.6 fusion.79
  261.4 0.6 fusion.77
  263.5 0.6 fusion.75
  267.6 0.6 fusion.71
  269.7 0.6 fusion.69
  271.7 0.6 fusion.67
  273.8 0.6 fusion.65
  275.8 0.6 fusion.63
  278.0 0.6 fusion.61
  280.1 0.6 fusion.59
  282.2 1.0 fusion.14
  283.2 14.1 %all_gather.14 = bf16[65536]{0:T(1024)(128)(2,1)S(1)} all-gather(bf16[8192]{0:T(1024)(128)(2,1)S(1)} %get-tuple-element.1024), channel_id=1, replica_groups=mesh['ex'=4,'ft'=8] {'ft'}, dimensions={0}, use_global_device_ids=true | all-gather | bytes 147456 | tf_op jit(solution)/shard_map/all_gather | solution.py:40
  297.3 11.3 %all_gather.15 = bf16[262144]{0:T(1024)(128)(2,1)S(1)} all-gather(bf16[65536]{0:T(1024)(128)(2,1)S(1)} %all_gather.14), channel_id=1, replica_groups=mesh['ex'=4,'ft'=8] {'ex'}, dimensions={0}, use_global_device_ids=true | all-gather | bytes 655360 | tf_op jit(solution)/shard_map/all_gather | solution.py:43
  309.1 6.8 %fusion.13 = bf16[16,1]{0,1:T(2,128)(2,1)S(1)} fusion(bf16[262144,1]{0,1:T(2,128)(2,1)S(1)} %reshape.1761, bf16[16,262144]{1,0:T(8,128)(2,1)} %param.169, s32[16]{0:T(128)S(1)} %copy-done.5), kind=kOutput, calls=%fused_computation.16 | convolution fusion | flops 8388704 | bytes 8912992 | tf_op jit(solution)/shard_map/dot_general | solution.py:41
  315.9 2.4 fusion.110
  318.4 51.6 %all-reduce.13.cloned.1.call-done = f32[262144]{0:T(1024)} async-done(((f32[262144]{0:T(1024)}), f32[262144]{0:T(1024)}) %all-reduce.13.cloned.1.call-update) | async-done | bytes 1048592
  370.0 1.7 dynamic-slice.494
  371.8 55.8 %all-reduce.15.cloned.1.call-done = f32[65536]{0:T(1024)} async-done(((f32[65536]{0:T(1024)}), f32[65536]{0:T(1024)}) %all-reduce.15.cloned.1.call-update) | async-done | bytes 262160
  427.6 0.8 fusion.103
  428.4 1.1 concatenate.170
  429.4 1.4 fusion.111
  430.8 39.5 %psum.15 = f32[41,41]{1,0:T(8,128)S(1)} all-reduce(f32[41,41]{1,0:T(8,128)S(1)} %fusion.111), channel_id=1, replica_groups=mesh['ex'=4,'ft'=8] {'ex','ft'}, use_global_device_ids=true, to_apply=%region_45.0 | all-reduce | flops 1681 | bytes 13448 | tf_op jit(solution)/shard_map/psum | solution.py:59
  470.3 0.7 fusion.105
  471.0 0.7 fusion.106
  472.3 0.7 fusion.16
  515.0 0.6 fusion.57
  516.9 0.6 fusion.55
  519.0 0.6 fusion.53
  521.1 0.6 fusion.51
  525.1 0.6 fusion.47
  527.3 0.6 fusion.45
  529.3 0.6 fusion.43
  531.4 0.6 fusion.41
  533.5 0.6 fusion.39
  535.6 0.6 fusion.37
  537.6 0.6 fusion.35
  541.7 0.6 fusion.31
  543.8 0.6 fusion.29
  545.9 0.6 fusion.27
  548.0 0.6 fusion.25
  554.2 0.6 fusion.19
  556.3 0.9 fusion.98
  557.2 0.6 add.678
  (172 shorter events, 42.6 us)
Async XLA Ops:
  7.2 27.4 %copy-start.5 = (s32[16]{0:T(128)S(1)}, s32[16]{0:T(128)}, u32[]{:S(2)}) copy-start(s32[16]{0:T(128)} %param.170) | copy-start | bytes 196
  7.2 89.5 %all-reduce.9.cloned.1.call-start = ((), (), s32[]{:S(2)}) async-start(), calls=%async_computation | async-start | bytes 2097152
  34.0 7.5 %slice-start = ((s8[8388608]{0:T(1024)(128)(4,1)}), s8[4194304]{0:T(1024)(128)(4,1)S(1)}, s32[]{:S(2)}) async-start(s8[8388608]{0:T(1024)(128)(4,1)} %bitcast.425), calls=%async_computation.4 | async-start | bytes 8388608
  34.6 7.0 %slice-start.1 = ((s8[8388608]{0:T(1024)(128)(4,1)}), s8[4194304]{0:T(1024)(128)(4,1)S(1)}, s32[]{:S(2)}) async-start(s8[8388608]{0:T(1024)(128)(4,1)} %bitcast.425), calls=%async_computation.5 | async-start | bytes 8388608
  41.6 2.5 copy-start.7
  44.0 54.4 %copy-start.6 = (u32[32]{0:T(128)S(1)}, u32[32]{0:T(128)}, u32[]{:S(2)}) copy-start(u32[32]{0:T(128)} %constant.1659) | copy-start | bytes 388
  44.0 55.0 %copy-start.8 = (f32[41]{0:T(128)S(1)}, f32[41]{0:T(128)}, u32[]{:S(2)}) copy-start(f32[41]{0:T(128)} %constant.1606.clone.1) | copy-start | bytes 496
  44.0 110.5 %copy-start.2 = (f32[8192]{0:T(1024)S(1)}, f32[8192]{0:T(1024)}, u32[]{:S(2)}) copy-start(f32[8192]{0:T(1024)} %param.171) | copy-start | bytes 98308
  44.0 111.2 %copy-start = (f32[20,8192]{1,0:T(8,128)S(1)}, f32[20,8192]{1,0:T(8,128)}, u32[]{:S(2)}) copy-start(f32[20,8192]{1,0:T(8,128)} %param.172) | copy-start | bytes 1966084
  44.0 111.2 %copy-start.1 = (f32[20,8192]{1,0:T(8,128)S(1)}, f32[20,8192]{1,0:T(8,128)}, u32[]{:S(2)}) copy-start(f32[20,8192]{1,0:T(8,128)} %param.173) | copy-start | bytes 1966084
  44.1 110.4 %all-reduce.11.cloned.1.call-start = ((), (), s32[]{:S(2)}) async-start(), calls=%async_computation.1 | async-start | bytes 524288
  98.4 99.8 %copy-start.4 = (f32[41,1]{1,0:T(8,128)S(1)}, f32[41,1]{1,0:T(8,128)}, u32[]{:S(2)}) copy-start(f32[41,1]{1,0:T(8,128)} %constant.1607.clone.1) | copy-start | bytes 496
  98.4 271.6 %all-reduce.13.cloned.1.call-start = ((), (), s32[]{:S(2)}) async-start(), calls=%async_computation.2 | async-start | bytes 2097152
  282.2 33.7 %slice-start.2 = ((s8[8388608]{0:T(1024)(128)(4,1)}), s8[4194304]{0:T(1024)(128)(4,1)S(1)}, s32[]{:S(2)}) async-start(s8[8388608]{0:T(1024)(128)(4,1)} %bitcast.427), calls=%async_computation.6 | async-start | bytes 8388608
  309.1 6.8 %slice-start.3 = ((s8[8388608]{0:T(1024)(128)(4,1)}), s8[4194304]{0:T(1024)(128)(4,1)S(1)}, s32[]{:S(2)}) async-start(s8[8388608]{0:T(1024)(128)(4,1)} %bitcast.427), calls=%async_computation.7 | async-start | bytes 8388608
  318.4 109.2 %all-reduce.15.cloned.1.call-start = ((), (), s32[]{:S(2)}) async-start(), calls=%async_computation.3 | async-start | bytes 524288
  557.2 0.6 copy-start.3
Sparse Core Ops, SparseCore 0:
  44.2 52.4 all-reduce.8
  99.0 55.4 all-reduce.10
  318.5 51.4 all-reduce.12
  372.2 55.4 all-reduce.14
where the time goes:
time: 566 us; the launch traced here: 564 us
  waiting for transfers between devices  213 us (38%)
  blocking collectives  130 us (23%)
  between operations  123 us (22%)
  other arithmetic  62.9 us (11%)
  matrix products  23.1 us (4%)
  local copies, waits for them, and re-layouts  11 us (2%)
    unnamed x8, waiting for transfers between devices  213 us
    psum x2, blocking collectives, per_device(): gram = lax.psum(local_gram(basis, basis), ('ex', 'ft'))  79 us
    all_gather x2, blocking collectives, per_device(): margins_quarter = lax.all_gather(half_weights, 'ft', axis=0, tiled=True)  29.8 us
    reduce_sum x40, other arithmetic, two_loop(): alpha = jnp.sum(delta * gram[:, index]) / gram[index, pairs + index]  24.3 us
    reduce_sum x40, other arithmetic, two_loop(): beta = jnp.sum(delta * gram[pairs + index, :]) / gram[index, pairs + index]  24.2 us
    all_gather x2, blocking collectives, per_device(): lax.all_gather(margins_quarter, 'ex', axis=0, tiled=True)  21.6 us
    dot_general x2, matrix products, per_device(): jnp.dot(features, lax.all_gather(margins_quarter, 'ex', axis=0, tiled=Tru...  13.7 us
  transfers between devices with their start and end apart: 4, of which 4 were waited for; matrix products, arithmetic and copies ran while one was open for 0% of the time, Pallas kernels for 0%

commit v1 on v0

v1 whole, which is shorter than its diff:
```python
import functools

import jax
import jax.numpy as jnp
from jax import lax
from jax.experimental import pallas as pl
from jax.experimental.pallas import tpu as pltpu
from jax.sharding import PartitionSpec as P

ITERS = 2
LANES = 128
MESH = pl.DeviceIdType.MESH
HIGH = lax.Precision.HIGHEST


def kernel(ne, nf, features, labels, weights, hist_s, hist_y, new_weights, direction,
           feat, s, y, wbf, wf, wg, sib_out, sib_in, own, chip_out, chip_in,
           grads, rows_out, rows_in, bf_out, bf_in, ac, bc, atc,
           feat_sem, hist_sem, ag_send, ag_recv, fw_send, fw_recv,
           sb_send, sb_recv, cp_send, cp_recv, ar_send, ar_recv, bf_send, bf_recv):
    nd = ne * nf
    chips = nd // 2
    examples = features.shape[0]
    rows = weights.shape[0]
    pairs = hist_s.shape[0]
    f32, bf16 = jnp.float32, jnp.bfloat16
    me = lax.axis_index("ex") * nf + lax.axis_index("ft")
    chip, core = me // 2, me % 2
    sibling = 2 * chip + (1 - core)

    def at(device):
        return (device // nf, device % nf)

    def remote(src, dst, send, recv, device):
        return pltpu.make_async_remote_copy(
            src_ref=src, dst_ref=dst, send_sem=send, recv_sem=recv,
            device_id=at(device), device_id_type=MESH)

    parts = feat_sem.shape[0]
    width = features.shape[1] // parts
    loads = [pltpu.make_async_copy(features.at[:, pl.ds(i * width, width)],
                                   feat.at[:, pl.ds(i * width, width)], feat_sem.at[i])
             for i in range(parts)]
    hist_loads = [pltpu.make_async_copy(hist_s, s, hist_sem.at[0]),
                  pltpu.make_async_copy(hist_y, y, hist_sem.at[1])]
    barrier = pltpu.get_barrier_semaphore()

    def greet(k, carry):
        pl.semaphore_signal(barrier, inc=1, device_id=at((me + k) % nd), device_id_type=MESH)
        return carry

    lax.fori_loop(1, nd, greet, 0)
    for copy in hist_loads + loads:
        copy.start()
    wbf[0] = weights[...].astype(bf16)
    wf[0] = weights[...]
    wg[0, me] = weights[...].astype(bf16)
    pl.semaphore_wait(barrier, nd - 1)

    def ag_copy(it, k):
        return remote(wbf.at[it], wg.at[it, me], ag_send.at[it, k], ag_recv.at[it, k],
                      2 * ((chip + k) % chips) + core)

    def fw_copy(it, k):
        block = 2 * ((chip - k + chips) % chips) + core
        return remote(wbf.at[it] if isinstance(k, int) else wg.at[it, block],
                      wg.at[it, block], fw_send.at[it, k], fw_recv.at[it, k], sibling)

    def gather_start(it):
        fw_copy(it, 0).start()

        def go(k, carry):
            ag_copy(it, k).start()
            return carry

        lax.fori_loop(1, chips, go, 0)

    def dot_block(it, device, acc):
        for half in range(rows // 16):
            w16 = wg[it, device, pl.ds(half * 16, 16), :].astype(f32)
            start = pl.multiple_of((device * rows + half * 16) * LANES, 16 * LANES)
            tile = feat[:, pl.ds(start, 16 * LANES)]
            for r in range(16):
                acc = acc + tile[:, r * LANES:(r + 1) * LANES].astype(f32) * w16[r:r + 1, :]
        return acc

    bits = bf_out.shape[0] - 1

    def bf_copy(b):
        step = 2 ** b
        partner = me + step * (1 - 2 * ((me // step) % 2))
        return remote(bf_out.at[b], bf_in.at[b], bf_send.at[b], bf_recv.at[b], partner)

    progress = [0]

    def advance():
        b = progress[0]
        if b < bits:
            bf_copy(b).wait()
            bf_out[b + 1] = bf_out[b] + bf_in[b]
            if b + 1 < bits:
                bf_copy(b + 1).start()
            progress[0] = b + 1

    sub = lax.broadcasted_iota(jnp.int32, (pairs, LANES), 0)
    lane = lax.broadcasted_iota(jnp.int32, (pairs, LANES), 1)

    def to_row(acc, offset):
        col = jnp.sum(acc, axis=1, keepdims=True)
        return jnp.sum(jnp.where(lane == sub + offset, col, 0.0), axis=0, keepdims=True)

    def to_col(row, offset):
        col = jnp.sum(jnp.where(lane == sub + offset, row, 0.0), axis=1, keepdims=True)
        return jnp.broadcast_to(col, (pairs, LANES))

    def all_sub(col):
        return jnp.broadcast_to(jnp.sum(col, axis=0, keepdims=True), (pairs, LANES))

    def spread(col, k):
        return jnp.broadcast_to(col[k:k + 1, :], (pairs, LANES))

    def ar_copy(it, k):
        return remote(rows_out.at[it], rows_in.at[it, k], ar_send.at[it, k], ar_recv.at[it, k],
                      (me + k) % nd)

    gather_start(0)
    hist_loads[0].wait()
    hist_loads[1].wait()

    chunk = min(1024, rows * LANES)
    contract = (((1,), (1,)), ((), ()))

    def products(i, sums):
        a = s[:, pl.ds(pl.multiple_of(i * chunk, chunk), chunk)]
        b = y[:, pl.ds(pl.multiple_of(i * chunk, chunk), chunk)]
        dot = functools.partial(lax.dot_general, dimension_numbers=contract, precision=HIGH,
                                preferred_element_type=f32)
        return (sums[0] + dot(a, b), sums[1] + dot(b, a), sums[2] + dot(b, b))

    zero = jnp.zeros((pairs, pairs), f32)
    sy, ys, yy = lax.fori_loop(0, rows * LANES // chunk, products, (zero, zero, zero))
    pad = jnp.zeros((pairs, LANES - 3 * pairs), f32)
    bf_out[0] = jnp.concatenate([sy, ys, yy, pad], axis=1)
    bf_copy(0).start()
    for copy in loads:
        copy.wait()

    for it in range(ITERS):
        acc = dot_block(it, me, jnp.zeros((examples, LANES), f32))

        def direct(k, acc):
            ag_copy(it, k).wait_recv()
            fw_copy(it, k).start()
            return dot_block(it, 2 * ((chip - k + chips) % chips) + core, acc)

        acc = lax.fori_loop(1, chips, direct, acc)
        advance()

        def forwarded(k, acc):
            fw_copy(it, k).wait_recv()
            return dot_block(it, 2 * ((chip - k + chips) % chips) + 1 - core, acc)

        fw_copy(it, 0).wait_recv()
        acc = dot_block(it, sibling, acc)
        acc = lax.fori_loop(1, chips, forwarded, acc)
        advance()
        margin = jnp.sum(acc, axis=1, keepdims=True)
        wide = 16 * examples
        on_diag = (lax.broadcasted_iota(jnp.int32, (examples, examples), 0)
                   == lax.broadcasted_iota(jnp.int32, (examples, examples), 1))
        label = jnp.sum(jnp.where(on_diag, labels[...].astype(f32), 0.0), axis=1, keepdims=True)
        resid = (1.0 / (1.0 + jnp.exp(-margin)) - label).astype(bf16).astype(f32)
        esub = lax.broadcasted_iota(jnp.int32, (examples, wide), 0)
        elane = lax.broadcasted_iota(jnp.int32, (examples, wide), 1)
        flat = jnp.sum(jnp.where(elane % examples == esub, resid, 0.0), axis=0, keepdims=True)
        gsub = lax.broadcasted_iota(jnp.int32, (16, wide), 0)
        glane = lax.broadcasted_iota(jnp.int32, (16, wide), 1)
        select = jnp.where(glane // examples == gsub, flat, 0.0).astype(bf16)

        def terms(device, part):
            start = pl.multiple_of((device * rows + part * 16) * LANES, 16 * LANES)
            tile = feat[:, pl.ds(start, 16 * LANES)]
            stack = jnp.concatenate(
                [tile[:, r * LANES:(r + 1) * LANES] for r in range(16)], axis=0)
            return jnp.dot(select, stack, preferred_element_type=f32)

        def sb_copy(k):
            return remote(sib_out.at[it, k], sib_in.at[it, k], sb_send.at[it, k],
                          sb_recv.at[it, k], sibling)

        def cp_copy(k):
            return remote(chip_out.at[it, k], chip_in.at[it, k], cp_send.at[it, k],
                          cp_recv.at[it, k], 2 * ((chip + k) % chips) + core)

        def compute(k):
            target = 2 * ((chip + k) % chips)
            for part in range(rows // 16):
                sib_out[it, k, pl.ds(part * 16, 16), :] = terms(target + 1 - core, part).astype(bf16)
            sb_copy(k).start()
            for part in range(rows // 16):
                own[k, pl.ds(part * 16, 16), :] = terms(target + core, part)

        def relay(k):
            sb_copy(k).wait_recv()
            chip_out[it, k] = (own[k] + sib_in[it, k].astype(f32)).astype(bf16)
            cp_copy(k).start()

        lag = min(3, chips - 1)

        def ahead(k, carry):
            compute(k)
            return carry

        def both(k, carry):
            compute(k)
            relay(k - lag)
            return carry

        def behind(k, carry):
            relay(k)
            return carry

        lax.fori_loop(1, 1 + lag, ahead, 0)
        lax.fori_loop(1 + lag, chips, both, 0)
        compute(0)
        lax.fori_loop(chips - lag, chips, behind, 0)
        advance()
        sb_copy(0).wait_recv()
        total = own[0] + sib_in[it, 0].astype(f32)

        def collect(k, total):
            cp_copy(k).wait_recv()
            return total + chip_in[it, k].astype(f32)

        total = lax.fori_loop(1, chips, collect, total)
        advance()
        w = wf[it]
        grad = total + 0.1 * w
        grads[it] = grad

        if it > 0:
            grads[ITERS + it] = grad - grads[it - 1]
            wf[ITERS + it] = w - wf[it - 1]
            for r in range(rows):
                s[0:1, r * LANES:(r + 1) * LANES] = wf[ITERS + it, r:r + 1, :]
                y[0:1, r * LANES:(r + 1) * LANES] = grads[ITERS + it, r:r + 1, :]
        accs = [jnp.zeros((pairs, LANES), f32) for _ in range(4 if it > 0 else 2)]
        for r in range(rows):
            st = s[:, r * LANES:(r + 1) * LANES]
            yt = y[:, r * LANES:(r + 1) * LANES]
            g = grads[it, r:r + 1, :]
            accs[0] = accs[0] + st * g
            accs[1] = accs[1] + yt * g
            if it > 0:
                dg = grads[ITERS + it, r:r + 1, :]
                accs[2] = accs[2] + st * dg
                accs[3] = accs[3] + yt * dg
        packed = to_row(accs[0], 0)
        for i in range(1, len(accs)):
            packed = packed + to_row(accs[i], i * pairs)
        rows_out[it] = packed
        rows_in[it, 0] = packed

        def ar_start(k, carry):
            ar_copy(it, k).start()
            return carry

        def ar_wait(k, carry):
            ar_copy(it, k).wait_recv()
            return carry

        lax.fori_loop(1, nd, ar_start, 0)
        if it == 0:
            while progress[0] < bits:
                advance()
            gram = bf_out[bits]
            diag = to_col(gram, 0)
            dinv = 1.0 / diag
            for k in range(pairs):
                col = jnp.broadcast_to(gram[:, k:k + 1], (pairs, LANES))
                ac[k] = jnp.where(sub < k, col * dinv, 0.0)
                col = jnp.broadcast_to(gram[:, pairs + k:pairs + k + 1], (pairs, LANES))
                atc[k] = jnp.where(sub > k, col * dinv, 0.0)
                bc[k] = jnp.broadcast_to(gram[:, 2 * pairs + k:2 * pairs + k + 1], (pairs, LANES))
            last = pairs - 1
            gamma = spread(diag, last) / spread(bc[last], last)
        lax.fori_loop(1, nd, ar_wait, 0)
        summed = jnp.sum(rows_in[it], axis=0)
        p, q = to_col(summed, 0), to_col(summed, pairs)

        first = sub == 0
        if it > 0:
            sdy, ydy = to_col(summed, 2 * pairs), to_col(summed, 3 * pairs)
            diag = jnp.where(first, sdy, diag)
            dinv = 1.0 / diag
            gamma = spread(sdy, 0) / spread(ydy, 0)
        t, v = -p * dinv, q
        if it > 0:
            a = spread(t, 0)
            t = t - a * jnp.where(first, 0.0, sdy * dinv)
            v = v + a * ydy
        for k in reversed(range(min(it, 1), pairs)):
            a = spread(t, k)
            column = ac[k]
            if it > 0:
                column = jnp.where(first, 0.0, column)
            t = t - a * column
            v = v + a * bc[k]
        if it > 0:
            v = jnp.where(first, q + all_sub(t * ydy), v)
        u = t + gamma * v * dinv
        for k in range(min(it, 1), pairs):
            u = u - spread(u, k) * atc[k]
        if it > 0:
            u = jnp.where(first, u - all_sub(jnp.where(first, 0.0, u * sdy)) * dinv, u)
        cy = -gamma * t
        cg = gamma[0:1, :]
        for r in range(rows):
            st = s[:, r * LANES:(r + 1) * LANES]
            yt = y[:, r * LANES:(r + 1) * LANES]
            step = jnp.sum(st * u + yt * cy, axis=0, keepdims=True) - cg * grads[it, r:r + 1, :]
            direction[r:r + 1, :] = step
        w = w + direction[...]
        if it + 1 < ITERS:
            wf[it + 1] = w
            wbf[it + 1] = w.astype(bf16)
            wg[it + 1, me] = w.astype(bf16)
            gather_start(it + 1)
        else:
            new_weights[...] = w

        def drain_chips(k, carry):
            ag_copy(it, k).wait_send()
            fw_copy(it, k).wait_send()
            sb_copy(k).wait_send()
            cp_copy(k).wait_send()
            return carry

        def drain_all(k, carry):
            ar_copy(it, k).wait_send()
            return carry

        fw_copy(it, 0).wait_send()
        sb_copy(0).wait_send()
        lax.fori_loop(1, chips, drain_chips, 0)
        lax.fori_loop(1, nd, drain_all, 0)


def per_device(ne, nf, features, labels, start_weights, hist_s, hist_y):
    nd = ne * nf
    chips = nd // 2
    bits = nd.bit_length() - 1
    examples = features.shape[0]
    size = start_weights.shape[0]
    pairs = hist_s.shape[0]
    rows = size // LANES
    f32, bf16 = jnp.float32, jnp.bfloat16
    vmem, dma = pltpu.VMEM, pltpu.SemaphoreType.DMA
    block = jax.ShapeDtypeStruct((rows, LANES), f32)
    in_vmem = pl.BlockSpec(memory_space=pltpu.VMEM)
    in_hbm = pl.BlockSpec(memory_space=pl.ANY)
    out = pl.pallas_call(
        functools.partial(kernel, ne, nf),
        out_shape=(block, block),
        in_specs=[in_hbm, in_vmem, in_vmem, in_hbm, in_hbm],
        out_specs=(in_vmem, in_vmem),
        scratch_shapes=[
            vmem(features.shape, bf16),
            vmem(hist_s.shape, f32),
            vmem(hist_y.shape, f32),
            vmem((ITERS, rows, LANES), bf16),
            vmem((2 * ITERS, rows, LANES), f32),
            vmem((ITERS, nd, rows, LANES), bf16),
            vmem((ITERS, chips, rows, LANES), bf16),
            vmem((ITERS, chips, rows, LANES), bf16),
            vmem((chips, rows, LANES), f32),
            vmem((ITERS, chips, rows, LANES), bf16),
            vmem((ITERS, chips, rows, LANES), bf16),
            vmem((2 * ITERS, rows, LANES), f32),
            vmem((ITERS, 1, LANES), f32),
            vmem((ITERS, nd, 1, LANES), f32),
            vmem((bits + 1, pairs, LANES), f32),
            vmem((bits, pairs, LANES), f32),
            vmem((pairs, pairs, LANES), f32),
            vmem((pairs, pairs, LANES), f32),
            vmem((pairs, pairs, LANES), f32),
            dma((8,)), dma((2,)),
            dma((ITERS, chips)), dma((ITERS, chips)),
            dma((ITERS, chips)), dma((ITERS, chips)),
            dma((ITERS, chips)), dma((ITERS, chips)),
            dma((ITERS, chips)), dma((ITERS, chips)),
            dma((ITERS, nd)), dma((ITERS, nd)),
            dma((bits,)), dma((bits,)),
        ],
        compiler_params=pltpu.CompilerParams(collective_id=0, has_side_effects=True),
    )(features, labels.reshape(1, examples), start_weights.reshape(rows, LANES), hist_s, hist_y)
    return out[0].reshape(size), out[1].reshape(size)


def solution(mesh):
    return jax.shard_map(
        functools.partial(per_device, mesh.shape["ex"], mesh.shape["ft"]),
        mesh=mesh,
        in_specs=(
            P(("ex", "ft"), None),
            P(("ex", "ft")),
            P(("ex", "ft")),
            P(None, ("ex", "ft")),
            P(None, ("ex", "ft")),
        ),
        out_specs=(P(("ex", "ft")), P(("ex", "ft"))),
        check_vma=False,
    )
```

time: 566 us -> 66.5 us (0.12)
  waiting for transfers between devices: 213 us -> 0 us
  blocking collectives: 130 us -> 0 us
  between operations: 123 us -> 0.64 us
  other arithmetic: 62.9 us -> 0 us
  Pallas kernels: 0 us -> 62.8 us
  matrix products: 23.1 us -> 0 us
  local copies, waits for them, and re-layouts: 11 us -> 2.75 us
    unnamed x8 -> x0, waiting for transfers between devices: 213 us -> none
    psum x2 -> x0, blocking collectives: 79 us -> none  [per_device(): gram = lax.psum(local_gram(basis, basis), ('ex', 'ft'))]
    pallas_call x0 -> x1, Pallas kernels: none -> 62.8 us  [per_device(): pl.pallas_call(functools.partial(kernel, ne, nf), out_shape=(block, block...]
    all_gather x4 -> x0, blocking collectives: 51.4 us -> none  [the longest x2 29.8 us: per_device(): margins_quarter = lax.all_gather(half_weights, 'ft', axis=0, tiled=True)]
    reduce_sum x80 -> x0, other arithmetic: 48.4 us -> none  [the longest x40 24.3 us: two_loop(): alpha = jnp.sum(delta * gram[:, index]) / gram[index, pairs + index]]
    dot_general x8 -> x0, matrix products: 23.1 us -> none  [the longest x2 13.7 us: per_device(): jnp.dot(features, lax.all_gather(margins_quarter, 'ex', axis=0, tiled=Tru...]
    scatter-add x78 -> x0, other arithmetic: 11.5 us -> none  [the longest x40 5.77 us: two_loop(): delta = delta.at[index].add(alphas[index] - beta)]
  transfers between devices with their start and end apart: 4 -> 0, of which waited for: 4 -> 0; matrix products, arithmetic and copies ran while one was open for 0% -> 0% of each run, Pallas kernels for 0% -> 0%
where the time goes in v1:
time: 66.5 us; the launch traced here: 66.2 us
  Pallas kernels  62.8 us (94%)
  local copies, waits for them, and re-layouts  2.75 us (4%)
    pallas_call x1, Pallas kernels, per_device(): pl.pallas_call(functools.partial(kernel, ne, nf), out_shape=(block, block...  62.8 us
    unnamed x2, local copies, waits for them, and re-layouts  2.75 us

profile of v1, /device:TPU:0, one launch (start us, length us, event | category | flops | bytes accessed | tf_op | source)
XLA Modules:
  0.0 66.2 jit_solution(12077570888608224903)
XLA Ops:
  0.6 62.8 %shard_map.68 = (f32[64,128]{1,0:T(8,128)}, f32[64,128]{1,0:T(8,128)}) custom-call(bf16[16,262144]{1,0:T(8,128)(2,1)} %features.1, s32[1,16]{1,0:T(1,128)} %bitcast.7, f32[64,128]{1,0:T(8,128)} %bitcast.4, f32[20,8192]{1,0:T(8,128)} %hist_s.1, f32[20,8192]{1,0:T(8,128)} %hist_y.1), custom_call_target="tpu_custom_call" | custom-call | tf_op jit(solution)/shard_map/pallas_call | solution.py:362
  63.5 1.4 %copy.9 = f32[8192]{0:T(1024)} copy(f32[8192]{0:T(1024)} %bitcast.6) | data formatting | bytes 65536
  64.8 1.4 %copy.10 = f32[8192]{0:T(1024)} copy(f32[8192]{0:T(1024)} %bitcast.5) | data formatting | bytes 65536

commit v2 on v1

--- a/solution.py
+++ b/solution.py
@@ -13,8 +13,11 @@
 HIGH = lax.Precision.HIGHEST
 
 
-def kernel(ne, nf, features, labels, weights, hist_s, hist_y, new_weights, direction,
-           feat, s, y, wbf, wf, wg, sib_out, sib_in, own, chip_out, chip_in,
+GROUPS = 4
+
+
+def kernel(ne, nf, features, labels_hbm, weights, hist_s, hist_y, new_weights, direction,
+           feat, s, y, labels, wbf, wf, wg, sib_out, sib_in, own, chip_out, chip_in,
            grads, rows_out, rows_in, bf_out, bf_in, ac, bc, atc,
            feat_sem, hist_sem, ag_send, ag_recv, fw_send, fw_recv,
            sb_send, sb_recv, cp_send, cp_recv, ar_send, ar_recv, bf_send, bf_recv):
@@ -36,6 +39,14 @@
             src_ref=src, dst_ref=dst, send_sem=send, recv_sem=recv,
             device_id=at(device), device_id_type=MESH)
 
+    barrier = pltpu.get_barrier_semaphore()
+
+    def greet(k, carry):
+        pl.semaphore_signal(barrier, inc=1, device_id=at((me + k) % nd), device_id_type=MESH)
+        return carry
+
+    lax.fori_loop(1, nd, greet, 0)
+
     parts = feat_sem.shape[0]
     width = features.shape[1] // parts
     loads = [pltpu.make_async_copy(features.at[:, pl.ds(i * width, width)],
@@ -43,41 +54,42 @@
              for i in range(parts)]
     hist_loads = [pltpu.make_async_copy(hist_s, s, hist_sem.at[0]),
                   pltpu.make_async_copy(hist_y, y, hist_sem.at[1])]
-    barrier = pltpu.get_barrier_semaphore()
-
-    def greet(k, carry):
-        pl.semaphore_signal(barrier, inc=1, device_id=at((me + k) % nd), device_id_type=MESH)
-        return carry
-
-    lax.fori_loop(1, nd, greet, 0)
-    for copy in hist_loads + loads:
+    small_loads = [pltpu.make_async_copy(weights, wf.at[0], hist_sem.at[2]),
+                   pltpu.make_async_copy(labels_hbm, labels, hist_sem.at[3])]
+    for copy in small_loads + hist_loads + loads:
         copy.start()
-    wbf[0] = weights[...].astype(bf16)
-    wf[0] = weights[...]
-    wg[0, me] = weights[...].astype(bf16)
+    for copy in small_loads:
+        copy.wait()
+    wbf[0] = wf[0].astype(bf16)
+    wg[0, core, 0] = wf[0].astype(bf16)
     pl.semaphore_wait(barrier, nd - 1)
 
     def ag_copy(it, k):
-        return remote(wbf.at[it], wg.at[it, me], ag_send.at[it, k], ag_recv.at[it, k],
+        return remote(wbf.at[it], wg.at[it, core, k], ag_send.at[it], ag_recv.at[it],
                       2 * ((chip + k) % chips) + core)
 
-    def fw_copy(it, k):
-        block = 2 * ((chip - k + chips) % chips) + core
-        return remote(wbf.at[it] if isinstance(k, int) else wg.at[it, block],
-                      wg.at[it, block], fw_send.at[it, k], fw_recv.at[it, k], sibling)
+    def ag_all(it):
+        slots = wg.at[it, core, pl.ds(1, chips - 1)]
+        return remote(slots, slots, ag_send.at[it], ag_recv.at[it], sibling)
+
+    def fw_copy(it):
+        return remote(wg.at[it, core], wg.at[it, core], fw_send.at[it], fw_recv.at[it], sibling)
+
+    def fw_wait(it):
+        return remote(wg.at[it, core], wg.at[it, 1 - core], fw_send.at[it], fw_recv.at[it],
+                      sibling)
 
     def gather_start(it):
-        fw_copy(it, 0).start()
-
         def go(k, carry):
             ag_copy(it, k).start()
             return carry
 
         lax.fori_loop(1, chips, go, 0)
 
-    def dot_block(it, device, acc):
+    def dot_block(it, half_chip, k, acc):
+        device = 2 * ((chip - k + chips) % chips) + half_chip
         for half in range(rows // 16):
-            w16 = wg[it, device, pl.ds(half * 16, 16), :].astype(f32)
+            w16 = wg[it, half_chip, k, pl.ds(half * 16, 16), :].astype(f32)
             start = pl.multiple_of((device * rows + half * 16) * LANES, 16 * LANES)
             tile = feat[:, pl.ds(start, 16 * LANES)]
             for r in range(16):
@@ -120,8 +132,12 @@
         return jnp.broadcast_to(col[k:k + 1, :], (pairs, LANES))
 
     def ar_copy(it, k):
-        return remote(rows_out.at[it], rows_in.at[it, k], ar_send.at[it, k], ar_recv.at[it, k],
+        return remote(rows_out.at[it], rows_in.at[it, k], ar_send.at[it], ar_recv.at[it],
                       (me + k) % nd)
+
+    def ar_all(it):
+        slots = rows_in.at[it, pl.ds(1, nd - 1)]
+        return remote(slots, slots, ar_send.at[it], ar_recv.at[it], sibling)
 
     gather_start(0)
     hist_loads[0].wait()
@@ -146,23 +162,17 @@
         copy.wait()
 
     for it in range(ITERS):
-        acc = dot_block(it, me, jnp.zeros((examples, LANES), f32))
-
-        def direct(k, acc):
-            ag_copy(it, k).wait_recv()
-            fw_copy(it, k).start()
-            return dot_block(it, 2 * ((chip - k + chips) % chips) + core, acc)
-
-        acc = lax.fori_loop(1, chips, direct, acc)
+        if it > 0:
+            wf[ITERS + it] = wf[it] - wf[it - 1]
+            for r in range(rows):
+                s[0:1, r * LANES:(r + 1) * LANES] = wf[ITERS + it, r:r + 1, :]
+        ag_all(it).wait_recv()
+        fw_copy(it).start()
         advance()
-
-        def forwarded(k, acc):
-            fw_copy(it, k).wait_recv()
-            return dot_block(it, 2 * ((chip - k + chips) % chips) + 1 - core, acc)
-
-        fw_copy(it, 0).wait_recv()
-        acc = dot_block(it, sibling, acc)
-        acc = lax.fori_loop(1, chips, forwarded, acc)
+        acc = lax.fori_loop(0, chips, lambda k, acc: dot_block(it, core, k, acc),
+                            jnp.zeros((examples, LANES), f32))
+        fw_wait(it).wait_recv()
+        acc = lax.fori_loop(0, chips, lambda k, acc: dot_block(it, 1 - core, k, acc), acc)
         advance()
         margin = jnp.sum(acc, axis=1, keepdims=True)
         wide = 16 * examples
@@ -184,55 +194,49 @@
                 [tile[:, r * LANES:(r + 1) * LANES] for r in range(16)], axis=0)
             return jnp.dot(select, stack, preferred_element_type=f32)
 
-        def sb_copy(k):
-            return remote(sib_out.at[it, k], sib_in.at[it, k], sb_send.at[it, k],
-                          sb_recv.at[it, k], sibling)
+        per = chips // GROUPS
+
+        def sb_copy(g):
+            slots = pl.ds(g * per, per)
+            return remote(sib_out.at[it, slots], sib_in.at[it, slots], sb_send.at[it, g],
+                          sb_recv.at[it, g], sibling)
 
         def cp_copy(k):
-            return remote(chip_out.at[it, k], chip_in.at[it, k], cp_send.at[it, k],
-                          cp_recv.at[it, k], 2 * ((chip + k) % chips) + core)
-
-        def compute(k):
+            return remote(chip_out.at[it, k], chip_in.at[it, k], cp_send.at[it],
+                          cp_recv.at[it], 2 * ((chip + k) % chips) + core)
+
+        def cp_all():
+            slots = chip_in.at[it, pl.ds(1, chips - 1)]
+            return remote(slots, slots, cp_send.at[it], cp_recv.at[it], sibling)
+
+        def compute(k, carry):
             target = 2 * ((chip + k) % chips)
             for part in range(rows // 16):
-                sib_out[it, k, pl.ds(part * 16, 16), :] = terms(target + 1 - core, part).astype(bf16)
-            sb_copy(k).start()
-            for part in range(rows // 16):
+                sib_out[it, k, pl.ds(part * 16, 16), :] = terms(target + 1 - core, part)
                 own[k, pl.ds(part * 16, 16), :] = terms(target + core, part)
-
-        def relay(k):
-            sb_copy(k).wait_recv()
-            chip_out[it, k] = (own[k] + sib_in[it, k].astype(f32)).astype(bf16)
+            return carry
+
+        def relay(k, carry):
+            chip_out[it, k] = (own[k] + sib_in[it, k]).astype(bf16)
             cp_copy(k).start()
-
-        lag = min(3, chips - 1)
-
-        def ahead(k, carry):
-            compute(k)
             return carry
 
-        def both(k, carry):
-            compute(k)
-            relay(k - lag)
-            return carry
-
-        def behind(k, carry):
-            relay(k)
-            return carry
-
-        lax.fori_loop(1, 1 + lag, ahead, 0)
-        lax.fori_loop(1 + lag, chips, both, 0)
-        compute(0)
-        lax.fori_loop(chips - lag, chips, behind, 0)
+        def relay_group(g):
+            sb_copy(g).wait_recv()
+            lax.fori_loop(max(1, g * per), (g + 1) * per, relay, 0)
+
+        order = list(reversed(range(GROUPS)))
+        for i, g in enumerate(order):
+            lax.fori_loop(g * per, (g + 1) * per, compute, 0)
+            sb_copy(g).start()
+            if i > 0:
+                relay_group(order[i - 1])
+        relay_group(order[-1])
         advance()
-        sb_copy(0).wait_recv()
-        total = own[0] + sib_in[it, 0].astype(f32)
-
-        def collect(k, total):
-            cp_copy(k).wait_recv()
-            return total + chip_in[it, k].astype(f32)
-
-        total = lax.fori_loop(1, chips, collect, total)
+        total = own[0] + sib_in[it, 0]
+        cp_all().wait_recv()
+        total = lax.fori_loop(
+            1, chips, lambda k, total: total + chip_in[it, k].astype(f32), total)
         advance()
         w = wf[it]
         grad = total + 0.1 * w
@@ -240,9 +244,7 @@
 
         if it > 0:
             grads[ITERS + it] = grad - grads[it - 1]
-            wf[ITERS + it] = w - wf[it - 1]
             for r in range(rows):
-                s[0:1, r * LANES:(r + 1) * LANES] = wf[ITERS + it, r:r + 1, :]
                 y[0:1, r * LANES:(r + 1) * LANES] = grads[ITERS + it, r:r + 1, :]
         accs = [jnp.zeros((pairs, LANES), f32) for _ in range(4 if it > 0 else 2)]
         for r in range(rows):
@@ -265,10 +267,6 @@
             ar_copy(it, k).start()
             return carry
 
-        def ar_wait(k, carry):
-            ar_copy(it, k).wait_recv()
-            return carry
-
         lax.fori_loop(1, nd, ar_start, 0)
         if it == 0:
             while progress[0] < bits:
@@ -284,7 +282,7 @@
                 bc[k] = jnp.broadcast_to(gram[:, 2 * pairs + k:2 * pairs + k + 1], (pairs, LANES))
             last = pairs - 1
             gamma = spread(diag, last) / spread(bc[last], last)
-        lax.fori_loop(1, nd, ar_wait, 0)
+        ar_all(it).wait_recv()
         summed = jnp.sum(rows_in[it], axis=0)
         p, q = to_col(summed, 0), to_col(summed, pairs)
 
@@ -319,31 +317,28 @@
             st = s[:, r * LANES:(r + 1) * LANES]
             yt = y[:, r * LANES:(r + 1) * LANES]
             step = jnp.sum(st * u + yt * cy, axis=0, keepdims=True) - cg * grads[it, r:r + 1, :]
-            direction[r:r + 1, :] = step
-        w = w + direction[...]
+            grads[ITERS, r:r + 1, :] = step
+        w = w + grads[ITERS]
         if it + 1 < ITERS:
             wf[it + 1] = w
             wbf[it + 1] = w.astype(bf16)
-            wg[it + 1, me] = w.astype(bf16)
+            wg[it + 1, core, 0] = w.astype(bf16)
             gather_start(it + 1)
         else:
             new_weights[...] = w
-
-        def drain_chips(k, carry):
-            ag_copy(it, k).wait_send()
-            fw_copy(it, k).wait_send()
-            sb_copy(k).wait_send()
-            cp_copy(k).wait_send()
-            return carry
-
-        def drain_all(k, carry):
-            ar_copy(it, k).wait_send()
-            return carry
-
-        fw_copy(it, 0).wait_send()
-        sb_copy(0).wait_send()
-        lax.fori_loop(1, chips, drain_chips, 0)
-        lax.fori_loop(1, nd, drain_all, 0)
+            direction[...] = grads[ITERS]
+
+        ag_all(it).wait_send()
+        fw_copy(it).wait_send()
+        cp_all().wait_send()
+        ar_all(it).wait_send()
+        for g in range(GROUPS):
+            sb_copy(g).wait_send()
+
+
+def finish(w, d, w_out, d_out):
+    w_out[...] = w[...]
+    d_out[...] = d[...]
 
 
 def per_device(ne, nf, features, labels, start_weights, hist_s, hist_y):
@@ -362,17 +357,18 @@
     out = pl.pallas_call(
         functools.partial(kernel, ne, nf),
         out_shape=(block, block),
-        in_specs=[in_hbm, in_vmem, in_vmem, in_hbm, in_hbm],
+        in_specs=[in_hbm] * 5,
         out_specs=(in_vmem, in_vmem),
         scratch_shapes=[
             vmem(features.shape, bf16),
             vmem(hist_s.shape, f32),
             vmem(hist_y.shape, f32),
+            vmem((1, examples), jnp.int32),
             vmem((ITERS, rows, LANES), bf16),
             vmem((2 * ITERS, rows, LANES), f32),
-            vmem((ITERS, nd, rows, LANES), bf16),
-            vmem((ITERS, chips, rows, LANES), bf16),
-            vmem((ITERS, chips, rows, LANES), bf16),
+            vmem((ITERS, 2, chips, rows, LANES), bf16),
+            vmem((ITERS, chips, rows, LANES), f32),
+            vmem((ITERS, chips, rows, LANES), f32),
             vmem((chips, rows, LANES), f32),
             vmem((ITERS, chips, rows, LANES), bf16),
             vmem((ITERS, chips, rows, LANES), bf16),
@@ -384,16 +380,18 @@
             vmem((pairs, pairs, LANES), f32),
             vmem((pairs, pairs, LANES), f32),
             vmem((pairs, pairs, LANES), f32),
-            dma((8,)), dma((2,)),
-            dma((ITERS, chips)), dma((ITERS, chips)),
-            dma((ITERS, chips)), dma((ITERS, chips)),
-            dma((ITERS, chips)), dma((ITERS, chips)),
-            dma((ITERS, chips)), dma((ITERS, chips)),
-            dma((ITERS, nd)), dma((ITERS, nd)),
+            dma((8,)), dma((4,)),
+            dma((ITERS,)), dma((ITERS,)),
+            dma((ITERS,)), dma((ITERS,)),
+            dma((ITERS, GROUPS)), dma((ITERS, GROUPS)),
+            dma((ITERS,)), dma((ITERS,)),
+            dma((ITERS,)), dma((ITERS,)),
             dma((bits,)), dma((bits,)),
         ],
         compiler_params=pltpu.CompilerParams(collective_id=0, has_side_effects=True),
     )(features, labels.reshape(1, examples), start_weights.reshape(rows, LANES), hist_s, hist_y)
+    out = pl.pallas_call(finish, out_shape=(block, block), in_specs=[in_vmem] * 2,
+                         out_specs=(in_vmem, in_vmem))(*out)
     return out[0].reshape(size), out[1].reshape(size)
 
 

time: 66.5 us -> 63.2 us (0.950)
  local copies, waits for them, and re-layouts: 2.75 us -> 0 us
    unnamed x2 -> x0, local copies, waits for them, and re-layouts: 2.75 us -> none
    pallas_call x1, Pallas kernels: 62.8 us -> 61 us  [per_device(): pl.pallas_call(functools.partial(kernel, ne, nf), out_shape=(block, block...]
    pallas_call x0 -> x1, Pallas kernels: none -> 1.4 us  [per_device(): pl.pallas_call(finish, out_shape=(block, block), in_specs=[in_vmem] * 2,...]
where the time goes in v2:
time: 63.2 us; the launch traced here: 63 us
  Pallas kernels  62.4 us (99%)
  between operations  0.64 us (1%)
    pallas_call x1, Pallas kernels, per_device(): pl.pallas_call(functools.partial(kernel, ne, nf), out_shape=(block, block...  61 us
    pallas_call x1, Pallas kernels, per_device(): pl.pallas_call(finish, out_shape=(block, block), in_specs=[in_vmem] * 2,...  1.4 us

profile of v2, /device:TPU:0, one launch (start us, length us, event | category | flops | bytes accessed | tf_op | source)
XLA Modules:
  0.0 63.0 jit_solution(8020828465252859654)
XLA Ops:
  0.6 61.0 %shard_map.68 = (f32[64,128]{1,0:T(8,128)}, f32[64,128]{1,0:T(8,128)}) custom-call(bf16[16,262144]{1,0:T(8,128)(2,1)} %features.1, s32[1,16]{1,0:T(1,128)} %bitcast.5, f32[64,128]{1,0:T(8,128)} %bitcast.4, f32[20,8192]{1,0:T(8,128)} %hist_s.1, f32[20,8192]{1,0:T(8,128)} %hist_y.1), custom_call_target="tpu_custom_call" | custom-call | tf_op jit(solution)/shard_map/pallas_call | solution.py:357
  61.6 1.4 %shard_map.69 = (f32[64,128]{1,0:T(8,128)}, f32[64,128]{1,0:T(8,128)}) custom-call(f32[64,128]{1,0:T(8,128)} %get-tuple-element.6.w, f32[64,128]{1,0:T(8,128)} %get-tuple-element.7.d), custom_call_target="tpu_custom_call" | custom-call | tf_op jit(solution)/shard_map/pallas_call | solution.py:393

commit v3 on v2

--- a/solution.py
+++ b/solution.py
@@ -64,27 +64,29 @@
     wg[0, core, 0] = wf[0].astype(bf16)
     pl.semaphore_wait(barrier, nd - 1)
 
+    per = chips // GROUPS
+
     def ag_copy(it, k):
-        return remote(wbf.at[it], wg.at[it, core, k], ag_send.at[it], ag_recv.at[it],
+        return remote(wbf.at[it], wg.at[it, core, k], ag_send.at[it], ag_recv.at[it, k // per],
                       2 * ((chip + k) % chips) + core)
 
-    def ag_all(it):
+    def ag_sent(it):
         slots = wg.at[it, core, pl.ds(1, chips - 1)]
-        return remote(slots, slots, ag_send.at[it], ag_recv.at[it], sibling)
-
-    def fw_copy(it):
-        return remote(wg.at[it, core], wg.at[it, core], fw_send.at[it], fw_recv.at[it], sibling)
-
-    def fw_wait(it):
-        return remote(wg.at[it, core], wg.at[it, 1 - core], fw_send.at[it], fw_recv.at[it],
-                      sibling)
+        return remote(slots, slots, ag_send.at[it], ag_recv.at[it, 0], sibling)
+
+    def ag_group(it, g):
+        first = max(1, g * per)
+        slots = wg.at[it, core, pl.ds(first, (g + 1) * per - first)]
+        return remote(slots, slots, ag_send.at[it], ag_recv.at[it, g], sibling)
+
+    def fw_copy(it, g, half_chip):
+        slots = pl.ds(g * per, per)
+        return remote(wg.at[it, core, slots], wg.at[it, half_chip, slots], fw_send.at[it, g],
+                      fw_recv.at[it, g], sibling)
 
     def gather_start(it):
-        def go(k, carry):
+        for k in range(1, chips):
             ag_copy(it, k).start()
-            return carry
-
-        lax.fori_loop(1, chips, go, 0)
 
     def dot_block(it, half_chip, k, acc):
         device = 2 * ((chip - k + chips) % chips) + half_chip
@@ -158,21 +160,33 @@
     pad = jnp.zeros((pairs, LANES - 3 * pairs), f32)
     bf_out[0] = jnp.concatenate([sy, ys, yy, pad], axis=1)
     bf_copy(0).start()
-    for copy in loads:
-        copy.wait()
 
     for it in range(ITERS):
         if it > 0:
             wf[ITERS + it] = wf[it] - wf[it - 1]
             for r in range(rows):
                 s[0:1, r * LANES:(r + 1) * LANES] = wf[ITERS + it, r:r + 1, :]
-        ag_all(it).wait_recv()
-        fw_copy(it).start()
-        advance()
-        acc = lax.fori_loop(0, chips, lambda k, acc: dot_block(it, core, k, acc),
-                            jnp.zeros((examples, LANES), f32))
-        fw_wait(it).wait_recv()
-        acc = lax.fori_loop(0, chips, lambda k, acc: dot_block(it, 1 - core, k, acc), acc)
+        acc = jnp.zeros((examples, LANES), f32)
+
+        def margins(g, half_chip, acc):
+            return lax.fori_loop(g * per, (g + 1) * per,
+                                 lambda k, acc: dot_block(it, half_chip, k, acc), acc)
+
+        for g in range(GROUPS):
+            if per > 1 or g > 0:
+                ag_group(it, g).wait_recv()
+            fw_copy(it, g, core).start()
+            if it == 0 and g == 0:
+                for copy in loads:
+                    copy.wait()
+            acc = margins(g, core, acc)
+            if g > 0:
+                fw_copy(it, g - 1, 1 - core).wait_recv()
+                acc = margins(g - 1, 1 - core, acc)
+            if g % 2 == 1:
+                advance()
+        fw_copy(it, GROUPS - 1, 1 - core).wait_recv()
+        acc = margins(GROUPS - 1, 1 - core, acc)
         advance()
         margin = jnp.sum(acc, axis=1, keepdims=True)
         wide = 16 * examples
@@ -193,8 +207,6 @@
             stack = jnp.concatenate(
                 [tile[:, r * LANES:(r + 1) * LANES] for r in range(16)], axis=0)
             return jnp.dot(select, stack, preferred_element_type=f32)
-
-        per = chips // GROUPS
 
         def sb_copy(g):
             slots = pl.ds(g * per, per)
@@ -267,7 +279,11 @@
             ar_copy(it, k).start()
             return carry
 
-        lax.fori_loop(1, nd, ar_start, 0)
+        if nd <= 32:
+            for k in range(1, nd):
+                ar_copy(it, k).start()
+        else:
+            lax.fori_loop(1, nd, ar_start, 0)
         if it == 0:
             while progress[0] < bits:
                 advance()
@@ -328,11 +344,11 @@
             new_weights[...] = w
             direction[...] = grads[ITERS]
 
-        ag_all(it).wait_send()
-        fw_copy(it).wait_send()
+        ag_sent(it).wait_send()
         cp_all().wait_send()
         ar_all(it).wait_send()
         for g in range(GROUPS):
+            fw_copy(it, g, core).wait_send()
             sb_copy(g).wait_send()
 
 
@@ -381,8 +397,8 @@
             vmem((pairs, pairs, LANES), f32),
             vmem((pairs, pairs, LANES), f32),
             dma((8,)), dma((4,)),
-            dma((ITERS,)), dma((ITERS,)),
-            dma((ITERS,)), dma((ITERS,)),
+            dma((ITERS,)), dma((ITERS, GROUPS)),
+            dma((ITERS, GROUPS)), dma((ITERS, GROUPS)),
             dma((ITERS, GROUPS)), dma((ITERS, GROUPS)),
             dma((ITERS,)), dma((ITERS,)),
             dma((ITERS,)), dma((ITERS,)),

time: 63.2 us -> 63.9 us (1.011)
  Pallas kernels: 62.4 us -> 63.1 us
    pallas_call x1, Pallas kernels: 61 us -> 61.7 us  [per_device(): pl.pallas_call(functools.partial(kernel, ne, nf), out_shape=(block, block...]
where the time goes in v3:
time: 63.9 us; the launch traced here: 63.7 us
  Pallas kernels  63.1 us (99%)
  between operations  0.64 us (1%)
    pallas_call x1, Pallas kernels, per_device(): pl.pallas_call(functools.partial(kernel, ne, nf), out_shape=(block, block...  61.7 us
    pallas_call x1, Pallas kernels, per_device(): pl.pallas_call(finish, out_shape=(block, block), in_specs=[in_vmem] * 2,...  1.4 us

profile of v3, /device:TPU:0, one launch (start us, length us, event | category | flops | bytes accessed | tf_op | source)
XLA Modules:
  0.0 63.7 jit_solution(12079868068445775593)
XLA Ops:
  0.6 61.7 %shard_map.68 = (f32[64,128]{1,0:T(8,128)}, f32[64,128]{1,0:T(8,128)}) custom-call(bf16[16,262144]{1,0:T(8,128)(2,1)} %features.1, s32[1,16]{1,0:T(1,128)} %bitcast.5, f32[64,128]{1,0:T(8,128)} %bitcast.4, f32[20,8192]{1,0:T(8,128)} %hist_s.1, f32[20,8192]{1,0:T(8,128)} %hist_y.1), custom_call_target="tpu_custom_call" | custom-call | tf_op jit(solution)/shard_map/pallas_call | solution.py:373
  62.3 1.4 %shard_map.69 = (f32[64,128]{1,0:T(8,128)}, f32[64,128]{1,0:T(8,128)}) custom-call(f32[64,128]{1,0:T(8,128)} %get-tuple-element.6.w, f32[64,128]{1,0:T(8,128)} %get-tuple-element.7.d), custom_call_target="tpu_custom_call" | custom-call | tf_op jit(solution)/shard_map/pallas_call | solution.py:409

commit v4 on v3

--- a/solution.py
+++ b/solution.py
@@ -30,6 +30,13 @@
     me = lax.axis_index("ex") * nf + lax.axis_index("ft")
     chip, core = me // 2, me % 2
     sibling = 2 * chip + (1 - core)
+
+    def flip(place, k, count):
+        bits = [2 ** i for i in range(count.bit_length() - 1)]
+        return sum(((place // b + k // b) % 2) * b for b in bits)
+
+    def mate(k):
+        return flip(chip, k, chips)
 
     def at(device):
         return (device // nf, device % nf)
@@ -68,7 +75,7 @@
 
     def ag_copy(it, k):
         return remote(wbf.at[it], wg.at[it, core, k], ag_send.at[it], ag_recv.at[it, k // per],
-                      2 * ((chip + k) % chips) + core)
+                      2 * mate(k) + core)
 
     def ag_sent(it):
         slots = wg.at[it, core, pl.ds(1, chips - 1)]
@@ -85,11 +92,11 @@
                       fw_recv.at[it, g], sibling)
 
     def gather_start(it):
-        for k in range(1, chips):
+        for k in reversed(range(1, chips)):
             ag_copy(it, k).start()
 
     def dot_block(it, half_chip, k, acc):
-        device = 2 * ((chip - k + chips) % chips) + half_chip
+        device = 2 * mate(k) + half_chip
         for half in range(rows // 16):
             w16 = wg[it, half_chip, k, pl.ds(half * 16, 16), :].astype(f32)
             start = pl.multiple_of((device * rows + half * 16) * LANES, 16 * LANES)
@@ -135,7 +142,7 @@
 
     def ar_copy(it, k):
         return remote(rows_out.at[it], rows_in.at[it, k], ar_send.at[it], ar_recv.at[it],
-                      (me + k) % nd)
+                      flip(me, k, nd))
 
     def ar_all(it):
         slots = rows_in.at[it, pl.ds(1, nd - 1)]
@@ -172,21 +179,22 @@
             return lax.fori_loop(g * per, (g + 1) * per,
                                  lambda k, acc: dot_block(it, half_chip, k, acc), acc)
 
-        for g in range(GROUPS):
+        order = list(reversed(range(GROUPS)))
+        for i, g in enumerate(order):
             if per > 1 or g > 0:
                 ag_group(it, g).wait_recv()
             fw_copy(it, g, core).start()
-            if it == 0 and g == 0:
+            if it == 0 and i == 0:
                 for copy in loads:
                     copy.wait()
             acc = margins(g, core, acc)
-            if g > 0:
-                fw_copy(it, g - 1, 1 - core).wait_recv()
-                acc = margins(g - 1, 1 - core, acc)
-            if g % 2 == 1:
+            if i > 0:
+                fw_copy(it, order[i - 1], 1 - core).wait_recv()
+                acc = margins(order[i - 1], 1 - core, acc)
+            if i % 2 == 1:
                 advance()
-        fw_copy(it, GROUPS - 1, 1 - core).wait_recv()
-        acc = margins(GROUPS - 1, 1 - core, acc)
+        fw_copy(it, order[-1], 1 - core).wait_recv()
+        acc = margins(order[-1], 1 - core, acc)
         advance()
         margin = jnp.sum(acc, axis=1, keepdims=True)
         wide = 16 * examples
@@ -215,14 +223,14 @@
 
         def cp_copy(k):
             return remote(chip_out.at[it, k], chip_in.at[it, k], cp_send.at[it],
-                          cp_recv.at[it], 2 * ((chip + k) % chips) + core)
+                          cp_recv.at[it], 2 * mate(k) + core)
 
         def cp_all():
             slots = chip_in.at[it, pl.ds(1, chips - 1)]
             return remote(slots, slots, cp_send.at[it], cp_recv.at[it], sibling)
 
         def compute(k, carry):
-            target = 2 * ((chip + k) % chips)
+            target = 2 * mate(k)
             for part in range(rows // 16):
                 sib_out[it, k, pl.ds(part * 16, 16), :] = terms(target + 1 - core, part)
                 own[k, pl.ds(part * 16, 16), :] = terms(target + core, part)
@@ -280,7 +288,7 @@
             return carry
 
         if nd <= 32:
-            for k in range(1, nd):
+            for k in reversed(range(1, nd)):
                 ar_copy(it, k).start()
         else:
             lax.fori_loop(1, nd, ar_start, 0)

time: 63.9 us -> 62.7 us (0.981)
  Pallas kernels: 63.1 us -> 61.8 us
    pallas_call x1, Pallas kernels: 61.7 us -> 60.4 us  [per_device(): pl.pallas_call(functools.partial(kernel, ne, nf), out_shape=(block, block...]
where the time goes in v4:
time: 62.7 us; the launch traced here: 62.5 us
  Pallas kernels  61.8 us (99%)
  between operations  0.64 us (1%)
    pallas_call x1, Pallas kernels, per_device(): pl.pallas_call(functools.partial(kernel, ne, nf), out_shape=(block, block...  60.4 us
    pallas_call x1, Pallas kernels, per_device(): pl.pallas_call(finish, out_shape=(block, block), in_specs=[in_vmem] * 2,...  1.4 us

profile of v4, /device:TPU:0, one launch (start us, length us, event | category | flops | bytes accessed | tf_op | source)
XLA Modules:
  0.0 62.5 jit_solution(9459291787235474685)
XLA Ops:
  0.6 60.4 %shard_map.68 = (f32[64,128]{1,0:T(8,128)}, f32[64,128]{1,0:T(8,128)}) custom-call(bf16[16,262144]{1,0:T(8,128)(2,1)} %features.1, s32[1,16]{1,0:T(1,128)} %bitcast.5, f32[64,128]{1,0:T(8,128)} %bitcast.4, f32[20,8192]{1,0:T(8,128)} %hist_s.1, f32[20,8192]{1,0:T(8,128)} %hist_y.1), custom_call_target="tpu_custom_call" | custom-call | tf_op jit(solution)/shard_map/pallas_call | solution.py:381
  61.1 1.4 %shard_map.69 = (f32[64,128]{1,0:T(8,128)}, f32[64,128]{1,0:T(8,128)}) custom-call(f32[64,128]{1,0:T(8,128)} %get-tuple-element.6.w, f32[64,128]{1,0:T(8,128)} %get-tuple-element.7.d), custom_call_target="tpu_custom_call" | custom-call | tf_op jit(solution)/shard_map/pallas_call | solution.py:417
